TPU v7x, 256 devices: a whole 4x4x8 slice. The times are simulated.
256 devices in a mesh: band: 8 (over y, core), col: 32 (over z, x).
Axes of the slice: x: 4, y: 4, z: 8, core: 2. Of those that a mesh axis runs over, the one named last changes fastest.
Arguments:
- source: bfloat16 [6, 4194304], P(None, ('band', 'col')), may hold values from -6 to 6
- weights: bfloat16 [65536, 128, 128], P(('band', 'col')), may hold values from -0.5 to 0.5
- source_block: int32 [65536], P(('band', 'col')), may hold values from 0 to 127
- owner_device: int32 [65536, 1], P(('band', 'col')), may hold values from 0 to 255, as said below
- target_tile: int32 [65536], P(('band', 'col')), may hold values from 0 to 112, as said below
- cutoff: int32 [512], P(('band', 'col')), may hold values from 1 to 511
Outputs:
- remapped: float32 [6, 512, 7200], P(None, 'band', 'col')
- filtered: float32 [6, 512, 7200], P(None, 'band', 'col')
Inputs may be any that keep to these rules, and one draw needn't show every extreme that they name: `owner_device`: owners are numbered band index times 32 plus col index. A device's blocks go only to owners in its own band or in the bands next to it. Among the 256 blocks of one device at most 6 share an owner; in every device exactly 6 do for some owner of its own band, and exactly 6 for some owner of each band next to its own; every device sends at least 4 blocks to each owner of its own band. `target_tile`: every tile of every owner receives at least one block.
All inputs are finite; a program needn't handle non-finite values.
Results may differ from a plain program's by a relative error of at most 0.0003.
Values sent between devices are 32-bit elements; how exact they have to be, the bound alone decides.
No kernel may reach another device: no remote copies, remote signals or barrier semaphores. Data moves between devices by JAX's collectives and lax.ppermute only.
A program may use at most 64 MiB of HBM per device.

v0:
```python
import jax
import jax.numpy as jnp
from jax import lax
from jax.experimental import pallas as pl
from jax.experimental.pallas import tpu as pltpu
from jax.sharding import PartitionSpec as P

NLON = 7200
KW = 512
TWO_PI = 6.283185307179586

LEV = 6
BLK = 128
COLS = 32
LON = NLON // COLS
LATB = 64
CAP = 6
SIDE_ROWS = CAP * LEV
ID_ROW = 3 * SIDE_ROWS
ROWS = ID_ROW + 4
WINDOW = 8
TILES = 120
P2_ROWS = 24
CHUNK = 128
CHUNKS = 2
AXES = True


def split2(x):
    hi = x.astype(jnp.bfloat16)
    lo = (x - hi.astype(jnp.float32)).astype(jnp.bfloat16)
    return hi, lo


def dot32(a, b):
    return jnp.dot(a, b, preferred_element_type=jnp.float32)


def place_kernel(sb_hbm, owner_hbm, tile_hbm, src_hbm, w_hbm, buf, w, src, sb, owners, tiles, marks, count, w_sem, in_sem):
    def chunk_copy(i):
        part = pl.ds(i * CHUNK, CHUNK)
        return pltpu.make_async_copy(w_hbm.at[part], w.at[part], w_sem.at[i])

    small = [
        pltpu.make_async_copy(owner_hbm, owners, in_sem.at[0]),
        pltpu.make_async_copy(sb_hbm, sb, in_sem.at[1]),
        pltpu.make_async_copy(tile_hbm, tiles, in_sem.at[2]),
        pltpu.make_async_copy(src_hbm, src, in_sem.at[3]),
    ]
    for copy in small:
        copy.start()
    for i in range(CHUNKS):
        chunk_copy(i).start()
    for i in range(3 * COLS):
        count[i] = 0
    buf[...] = jnp.zeros_like(buf)
    marks[...] = jnp.zeros_like(marks)
    for copy in small:
        copy.wait()
    band = lax.axis_index("band").astype(jnp.int32) if AXES else 3
    col = lax.axis_index("col").astype(jnp.int32) if AXES else 5
    first = (band - 1) * COLS
    odd = band % 2
    side_base = jnp.where(odd == 1, 0, 2 * SIDE_ROWS)
    side_step = jnp.where(odd == 1, SIDE_ROWS, -SIDE_ROWS)
    lane = (lax.broadcasted_iota(jnp.int32, (1, BLK), 1) - col % (COLS // 2) * WINDOW) * LEV

    def chunk(i, carry):
        chunk_copy(i).wait()
        for u in range(CHUNK):
            n = i * CHUNK + u
            key = owners[n] - first
            start = pl.multiple_of(sb[n] * BLK, BLK)
            value = dot32(src[:, pl.ds(start, BLK)], w[n])
            row = count[key]
            count[key] = row + LEV
            buf[key & (COLS - 1), pl.ds((key >> 5) * side_step + (side_base + row), LEV), :] = value
            mark = jnp.where(lane == row, tiles[n] + 1, 0)
            marks[pl.ds(key, 1), :] = marks[pl.ds(key, 1), :] + mark.astype(jnp.float32)
        return carry

    lax.fori_loop(0, CHUNKS, chunk, 0)
    below, above = marks[:COLS, :], marks[2 * COLS :, :]
    marks[:COLS, :] = jnp.where(odd == 1, below, above)
    marks[2 * COLS :, :] = pltpu.roll(jnp.where(odd == 1, above, below), WINDOW - CAP, 1)
    for key in range(3 * COLS):
        row = ID_ROW + key // COLS
        buf[key % COLS, row : row + 1, :] = marks[key : key + 1, :]


def place(source, weights, source_block, owners, target_tile, interpret=False):
    hbm = pl.BlockSpec(memory_space=pltpu.HBM)
    blocks = weights.shape[0]
    return pl.pallas_call(
        place_kernel,
        out_shape=pltpu.VMEM((COLS, ROWS, BLK), jnp.float32),
        in_specs=[hbm] * 5,
        out_specs=pl.BlockSpec(memory_space=pltpu.VMEM),
        scratch_shapes=[
            pltpu.VMEM(weights.shape, weights.dtype),
            pltpu.VMEM(source.shape, source.dtype),
            pltpu.SMEM((blocks,), jnp.int32),
            pltpu.SMEM((blocks,), jnp.int32),
            pltpu.SMEM((blocks,), jnp.int32),
            pltpu.VMEM((3 * COLS, BLK), jnp.float32),
            pltpu.SMEM((3 * COLS,), jnp.int32),
            pltpu.SemaphoreType.DMA((CHUNKS,)),
            pltpu.SemaphoreType.DMA((4,)),
        ],
        compiler_params=pltpu.CompilerParams(vmem_limit_bytes=58 << 20),
        cost_estimate=pl.CostEstimate(flops=100_000_000, bytes_accessed=10_000_000, transcendentals=0),
        interpret=interpret,
        name="place",
    )(source_block, owners, target_tile, source, weights)


def sum_side(side, got_ref, out_ref):
    begin = min(side * CAP, 3 * CAP - WINDOW) * LEV
    halves = []
    for half in range(2):
        at = half * (COLS // 2) * ROWS + ID_ROW + side
        marks = [got_ref[pl.ds(at + g * 8 * ROWS, 8, stride=ROWS), :] for g in range(2)]
        halves.append(jnp.sum(marks[0] + marks[1], axis=0, keepdims=True))
    ids = jnp.concatenate(halves, axis=1)
    tile = lax.broadcasted_iota(jnp.int32, (TILES, 2 * BLK), 0).astype(jnp.float32) + 1.0
    chooser = jnp.where(tile == ids, 1.0, 0.0).astype(jnp.bfloat16)
    for l in range(LEV):
        data = [got_ref[pl.ds(s * ROWS + begin + l, WINDOW, stride=LEV), :] for s in range(COLS)]
        both = dot32(chooser, jnp.concatenate(split2(jnp.concatenate(data, axis=0)), axis=1))
        out_ref[l * TILES : l * TILES + TILES, :] = both[:, :BLK] + both[:, BLK:]


def tile_sums(got, sides, interpret=False):
    def kernel(got_ref, *out_refs):
        for side, out_ref in zip(sides, out_refs):
            sum_side(side, got_ref, out_ref)

    return pl.pallas_call(
        kernel,
        out_shape=[jax.ShapeDtypeStruct((LEV * TILES, BLK), jnp.float32)] * len(sides),
        compiler_params=pltpu.CompilerParams(vmem_limit_bytes=24 << 20),
        cost_estimate=pl.CostEstimate(flops=100_000_000 * len(sides), bytes_accessed=1_000_000, transcendentals=0),
        interpret=interpret,
    )(got)


def by_row_kernel(own_ref, core_ref, chip_ref, out_ref, sums):
    sums[...] = own_ref[...] + core_ref[...] + chip_ref[...]
    lane = lax.broadcasted_iota(jnp.int32, (LEV, BLK), 1)
    for lat in range(LATB):
        for half in range(2):
            first, shift = divmod(lat * LON + half * BLK, BLK)
            value = sums[pl.ds(first, LEV, stride=TILES), :]
            if shift:
                later = sums[pl.ds(first + 1, LEV, stride=TILES), :]
                value = jnp.where(lane < BLK - shift, pltpu.roll(value, BLK - shift, 1), pltpu.roll(later, BLK - shift, 1))
            at = (lat % 2) * 2 * LEV + half * LEV
            out_ref[lat // 2, at : at + LEV, :] = value


def by_row(own, core, chip, interpret=False):
    return pl.pallas_call(
        by_row_kernel,
        out_shape=jax.ShapeDtypeStruct((COLS, P2_ROWS, BLK), jnp.float32),
        scratch_shapes=[pltpu.VMEM((LEV * TILES, BLK), jnp.float32)],
        compiler_params=pltpu.CompilerParams(vmem_limit_bytes=12 << 20),
        cost_estimate=pl.CostEstimate(flops=1_000_000, bytes_accessed=1_500_000, transcendentals=0),
        interpret=interpret,
        name="by_row",
    )(own, core, chip)


def stack_k(x):
    hi, lo = split2(x)
    return jnp.concatenate([hi, lo, hi], axis=0)


def filter_kernel(x_ref, f_ref, ft_ref, g_ref, gt_ref, tc_ref, ts_ref, gain_ref, out_ref):
    order = [p * 2 * LEV + h * LEV + l for p in range(2) for l in range(LEV) for h in range(2)]
    x = jnp.concatenate([x_ref[pl.ds(at, COLS, stride=P2_ROWS), :] for at in order], axis=1)
    tc, ts = tc_ref[...], ts_ref[...]
    y = dot32(f_ref[...], stack_k(x))
    rows = []
    for r in range(2 * LEV):
        re, im = y[:COLS, r * 256 : r * 256 + 256], y[COLS:, r * 256 : r * 256 + 256]
        rows.append(jnp.concatenate([re * tc + im * ts, im * tc - re * ts], axis=1))
    hi, lo = split2(jnp.concatenate(rows, axis=0))
    z = dot32(jnp.concatenate([hi, lo, hi], axis=1), g_ref[...]) * gain_ref[...]
    hi, lo = split2(z)
    middle = lax.broadcasted_iota(jnp.int32, z.shape, 1) // COLS == 1
    w = dot32(jnp.where(middle, lo.astype(jnp.float32), hi.astype(jnp.float32)).astype(jnp.bfloat16), gt_ref[...])
    cols = []
    for r in range(2 * LEV):
        part = w[r * COLS : r * COLS + COLS]
        re, im = part[:, :256], part[:, 256:]
        cols.append(jnp.concatenate([re * tc - im * ts, re * ts + im * tc], axis=0))
    out = dot32(ft_ref[...], stack_k(jnp.concatenate(cols, axis=1)))
    for i, at in enumerate(order):
        out_ref[pl.ds(at, COLS, stride=P2_ROWS), :] = out[:, i * BLK : i * BLK + BLK]


def zonal_filter(rows, tables, interpret=False):
    out = pl.pallas_call(
        filter_kernel,
        out_shape=jax.ShapeDtypeStruct((COLS * P2_ROWS, BLK), jnp.float32),
        compiler_params=pltpu.CompilerParams(vmem_limit_bytes=24 << 20),
        cost_estimate=pl.CostEstimate(flops=300_000_000, bytes_accessed=1_000_000, transcendentals=0),
        interpret=interpret,
        name="zonal",
    )(rows.reshape(COLS * P2_ROWS, BLK), *tables)
    return out.reshape(COLS, P2_ROWS, BLK)


def angles(zero, shape, factor, period):
    a = zero + lax.broadcasted_iota(jnp.int32, shape, 0)
    b = lax.broadcasted_iota(jnp.int32, shape, 1)
    phases = a * b * factor % period
    return phases.astype(jnp.float32) * (TWO_PI / period)


def three(x, axis):
    hi = lax.reduce_precision(x, 8, 7)
    return jnp.concatenate([hi, hi, x - hi], axis=axis).astype(jnp.bfloat16)


def zonal_tables(cutoff, zero):
    theta = angles(zero, (COLS, COLS), 1, COLS)
    f = jnp.concatenate([jnp.cos(theta), -jnp.sin(theta)], axis=0)
    turn = angles(zero, (COLS, 256), 1, NLON)
    tc, ts = jnp.cos(turn), jnp.sin(turn)
    phi = angles(zero, (KW // COLS, 256), COLS, NLON)
    inside = zero + lax.broadcasted_iota(jnp.int32, phi.shape, 1) < LON
    c, s = jnp.where(inside, jnp.cos(phi), 0.0), jnp.where(inside, jnp.sin(phi), 0.0)
    gt = jnp.concatenate([jnp.concatenate([c, s], axis=1), jnp.concatenate([-s, c], axis=1)], axis=0)
    g = jnp.concatenate([three(gt.T, 0)] * 3, axis=1)
    shape = (2, LEV, COLS, 3, 2, KW // COLS)
    k = zero + lax.broadcasted_iota(jnp.int32, shape, 2) + COLS * (zero + lax.broadcasted_iota(jnp.int32, shape, 5))
    gain = jnp.where(k == 0, 1.0, 2.0) / NLON
    gain = jnp.where(k <= cutoff.reshape(2, 1, 1, 1, 1, 1), gain, 0.0).reshape(2 * LEV * COLS, 3 * COLS)
    return three(f, 1), three(f.T, 1), g, three(gt, 0), tc, ts, gain


def lay_kernel(rows_ref, out_ref, low, high):
    for h, half in enumerate((low, high)):
        for p in range(2):
            for l in range(LEV):
                part = rows_ref[pl.ds(p * 2 * LEV + h * LEV + l, COLS, stride=P2_ROWS), :]
                half[pl.ds(l * LATB + p, COLS, stride=2), :] = part
    for l in range(LEV):
        out_ref[l, :, :BLK] = low[l * LATB : l * LATB + LATB, :]
        out_ref[l, :, BLK:] = high[l * LATB : l * LATB + LATB, : LON - BLK]


def by_latitude(rows, interpret=False):
    return pl.pallas_call(
        lay_kernel,
        out_shape=jax.ShapeDtypeStruct((LEV, LATB, LON), jnp.float32),
        scratch_shapes=[pltpu.VMEM((LEV * LATB, BLK), jnp.float32)] * 2,
        cost_estimate=pl.CostEstimate(flops=1_000_000, bytes_accessed=800_000, transcendentals=0),
        compiler_params=pltpu.CompilerParams(vmem_limit_bytes=8 << 20),
        interpret=interpret,
        name="lay",
    )(rows.reshape(COLS * P2_ROWS, BLK))


def exchange(array):
    return lax.all_to_all(array, "col", 0, 0, tiled=True)


def local(source, weights, source_block, owner_device, target_tile, cutoff):
    bands = lax.axis_size("band")
    got = exchange(place(source, weights, source_block, owner_device[:, 0], target_tile))
    got, cutoff, zero = lax.optimization_barrier((got.reshape(COLS * ROWS, BLK), cutoff, jnp.int32(0)))
    to_chip, to_core = tile_sums(got, (2, 0))
    pairs = [(i, i + 1 if i % 2 else i - 1) for i in range(1, bands - 1)]
    chip = lax.ppermute(to_chip, "band", pairs)
    core = lax.ppermute(to_core, "band", [(i, i ^ 1) for i in range(bands)])
    (own,) = tile_sums(got, (1,))
    rows = by_row(own, core, chip)
    remapped = by_latitude(rows)
    rows, remapped = lax.optimization_barrier((exchange(rows), remapped))
    rows = zonal_filter(rows, zonal_tables(cutoff, zero))
    filtered = by_latitude(exchange(rows))
    return (remapped, filtered)


def solution(mesh):
    in_specs = (
        P(None, ("band", "col")),
        P(("band", "col"), None, None),
        P(("band", "col")),
        P(("band", "col"), None),
        P(("band", "col")),
        P(("band", "col")),
    )
    out_specs = (P(None, "band", "col"), P(None, "band", "col"))
    return jax.shard_map(local, mesh=mesh, in_specs=in_specs, out_specs=out_specs, check_vma=False)
```

profile of v0, /device:TPU:8, one launch (start us, length us, event | category | flops | bytes accessed | tf_op | source)
XLA Modules:
  0.0 115.4 jit_solution(6784312612258017422)
XLA Ops:
  0.6 5.0 %place.1 = f32[32,112,128]{2,1,0:T(8,128)S(1)} custom-call(s32[256]{0:T(256)} %sb_hbm.1, s32[256]{0:T(256)} %bitcast.17, s32[256]{0:T(256)} %tile_hbm.1, bf16[6,16384]{1,0:T(8,128)(2,1)} %src_hbm.1, bf16[256,128,128]{2,1,0:T(8,128)(2,1)} %w_hbm.1), custom_call_target="tpu_custom_call" | custom-call | flops 100000000 | bytes 10000000 | tf_op jit(solution)/shard_map/place/pallas_call | solution.py:94
  5.6 56.9 %all_to_all.15 = f32[32,112,128]{2,1,0:T(8,128)S(1)} all-to-all(f32[32,112,128]{2,1,0:T(8,128)S(1)} %place.1), channel_id=1, replica_groups=mesh['band'=8,'col'=32] {'col'}, dimensions={0} | all-to-all | bytes 3670016 | tf_op jit(solution)/shard_map/all_to_all | solution.py:267
  62.5 0.0 copy-start
  62.5 0.1 fusion.22
  62.6 1.1 shard_map.78
  63.7 0.0 collective-permute-start
  63.7 2.4 %collective-permute-start.1 = (f32[720,128]{1,0:T(8,128)S(1)}, f32[720,128]{1,0:T(8,128)S(1)}, u32[]{:S(2)}, u32[]{:S(2)}) collective-permute-start(f32[720,128]{1,0:T(8,128)S(1)} %get-tuple-element.11), channel_id=1, source_target_pairs={{32,64},{64,32},{96,128},{128,96},{160,192},{192,160},{33,65},{65,... | collective-permute-start | bytes 1105928 | tf_op jit(solution)/shard_map/ppermute | solution.py:276
  66.2 0.2 sine_select_fusion
  66.4 0.7 maximum_maximum_fusion
  67.1 0.1 reduce-precision_convert_fusion.2
  67.2 1.2 %copy.11.g_ref = bf16[1536,96]{1,0:T(8,128)(2,1)S(1)} copy(bf16[1536,96]{0,1:T(8,128)(2,1)} %maximum_maximum_fusion) | data formatting | bytes 589824 | tf_op jit(solution)/shard_map/concatenate | solution.py:235
  68.4 0.1 copy.10.f_ref
  68.5 0.1 iota.62
  68.6 0.1 mul.58
  68.7 0.0 copy-done
  68.7 0.1 le.13
  68.7 0.1 le.14
  68.8 0.3 shard_map.77.own_ref
  69.1 0.0 collective-permute-done.core_ref
  69.1 3.4 %collective-permute-done.1.chip_ref = f32[720,128]{1,0:T(8,128)S(1)} collective-permute-done((f32[720,128]{1,0:T(8,128)S(1)}, f32[720,128]{1,0:T(8,128)S(1)}, u32[]{:S(2)}, u32[]{:S(2)}) %collective-permute-start.1) | collective-permute-done | bytes 368672 | tf_op jit(solution)/shard_map/ppermute | solution.py:276
  72.6 1.1 by_row.1
  73.7 4.7 %all-to-all-start.1 = ((f32[32,24,128]{2,1,0:T(8,128)}), f32[32,24,128]{2,1,0:T(8,128)S(1)}, u32[]{:S(2)}, u32[]{:S(2)}) async-start(f32[32,24,128]{2,1,0:T(8,128)} %by_row.1), calls=%async_computation.1 | async-start | bytes 786432 | tf_op jit(solution)/shard_map/all_to_all | solution.py:267
  78.4 0.1 pad_maximum_fusion.3.ft_ref
  78.5 0.2 fusion.6
  78.7 0.2 multiply_select_fusion.gain_ref
  78.9 1.8 %lay.2 = f32[6,64,225]{2,1,0:T(8,128)} custom-call(f32[768,128]{1,0:T(8,128)} %bitcast.2.rows_ref), custom_call_target="tpu_custom_call" | custom-call | flops 1000000 | bytes 800000 | tf_op jit(solution)/shard_map/lay/pallas_call | solution.py:255
  80.8 13.7 %all-to-all-done.1 = f32[32,24,128]{2,1,0:T(8,128)S(1)} async-done(((f32[32,24,128]{2,1,0:T(8,128)}), f32[32,24,128]{2,1,0:T(8,128)S(1)}, u32[]{:S(2)}, u32[]{:S(2)}) %all-to-all-start.1) | async-done | bytes 393248 | tf_op jit(solution)/shard_map/all_to_all | solution.py:267
  94.4 1.4 %zonal.1 = f32[768,128]{1,0:T(8,128)S(1)} custom-call(f32[768,128]{1,0:T(8,128)S(1)} %bitcast.15, bf16[64,96]{1,0:T(8,128)(2,1)S(1)} %copy.10.f_ref, bf16[32,192]{1,0:T(8,128)(2,1)S(1)} %pad_maximum_fusion.3.ft_ref, bf16[1536,96]{1,0:T(8,128)(2,1)S(1)} %copy.11.g_ref, bf16[96,512]{1,0:T(8,128)(2,1)S(1)} %pad_maximum_fusion.gt_ref, ...), custom_call_target="tpu_custom_call" | custom-call | flops 300000000 | bytes 1000000 | tf_op jit(solution)/shard_map/zonal/pallas_call | solution.py:203
  95.9 18.7 %all_to_all.16 = f32[32,24,128]{2,1,0:T(8,128)S(1)} all-to-all(f32[32,24,128]{2,1,0:T(8,128)S(1)} %bitcast.16), channel_id=1, replica_groups=mesh['band'=8,'col'=32] {'col'}, dimensions={0} | all-to-all | bytes 786432 | tf_op jit(solution)/shard_map/all_to_all | solution.py:267
  114.6 0.8 lay.3
  (11 shorter events, 0.1 us)
Async XLA Ops:
  62.5 6.2 %copy-start = (s32[2]{0:T(128)S(1)}, s32[2]{0:T(128)}, u32[]{:S(2)}) copy-start(s32[2]{0:T(128)} %param.11) | copy-start | bytes 28
  63.7 5.4 %collective-permute-start = (f32[720,128]{1,0:T(8,128)}, f32[720,128]{1,0:T(8,128)S(1)}, u32[]{:S(2)}, u32[]{:S(2)}) collective-permute-start(f32[720,128]{1,0:T(8,128)} %get-tuple-element.10), channel_id=1, source_target_pairs={{0,32},{32,0},{64,96},{96,64},{128,160},{160,128},{192,224},{224,1... | collective-permute-start | bytes 1105928 | tf_op jit(solution)/shard_map/ppermute | solution.py:277
  63.7 8.8 %collective-permute-start.1 = (f32[720,128]{1,0:T(8,128)S(1)}, f32[720,128]{1,0:T(8,128)S(1)}, u32[]{:S(2)}, u32[]{:S(2)}) collective-permute-start(f32[720,128]{1,0:T(8,128)S(1)} %get-tuple-element.11), channel_id=1, source_target_pairs={{32,64},{64,32},{96,128},{128,96},{160,192},{192,160},{33,65},{65,... | collective-permute-start | bytes 1105928 | tf_op jit(solution)/shard_map/ppermute | solution.py:276
  73.7 20.8 %all-to-all-start.1 = ((f32[32,24,128]{2,1,0:T(8,128)}), f32[32,24,128]{2,1,0:T(8,128)S(1)}, u32[]{:S(2)}, u32[]{:S(2)}) async-start(f32[32,24,128]{2,1,0:T(8,128)} %by_row.1), calls=%async_computation.1 | async-start | bytes 786432 | tf_op jit(solution)/shard_map/all_to_all | solution.py:267
where the time goes:
time: 116 us; the launch traced here: 115 us
  blocking collectives  75.6 us (65%)
  waiting for transfers between devices  17.1 us (15%)
  Pallas kernels  11.6 us (10%)
  starting transfers between devices  7.17 us (6%)
  local copies, waits for them, and re-layouts  1.59 us (1%)
  other arithmetic  1.59 us (1%)
    all_to_all x2, blocking collectives, exchange(): return lax.all_to_all(array, 'col', 0, 0, tiled=True)  75.6 us
    all_to_all x1, waiting for transfers between devices, exchange(): return lax.all_to_all(array, 'col', 0, 0, tiled=True)  13.7 us
    pallas_call x1, Pallas kernels, place(): pl.pallas_call(place_kernel, out_shape=pltpu.VMEM((COLS, ROWS, BLK), jnp....  4.98 us
    all_to_all x1, starting transfers between devices, exchange(): return lax.all_to_all(array, 'col', 0, 0, tiled=True)  4.73 us
    ppermute x1, waiting for transfers between devices, local(): chip = lax.ppermute(to_chip, 'band', pairs)  3.41 us
    pallas_call x2, Pallas kernels, by_latitude(): pl.pallas_call(lay_kernel, out_shape=jax.ShapeDtypeStruct((LEV, LATB, LON...  2.69 us
    ppermute x1, starting transfers between devices, local(): chip = lax.ppermute(to_chip, 'band', pairs)  2.44 us
  transfers between devices with their start and end apart: 3, of which 2 were waited for; matrix products, arithmetic and copies ran while one was open for 3% of the time, Pallas kernels for 2%

commit v1 on v0

--- a/solution.py
+++ b/solution.py
@@ -270,16 +270,19 @@
 def local(source, weights, source_block, owner_device, target_tile, cutoff):
     bands = lax.axis_size("band")
     got = exchange(place(source, weights, source_block, owner_device[:, 0], target_tile))
-    got, cutoff, zero = lax.optimization_barrier((got.reshape(COLS * ROWS, BLK), cutoff, jnp.int32(0)))
+    got = got.reshape(COLS * ROWS, BLK)
     to_chip, to_core = tile_sums(got, (2, 0))
+    to_chip, to_core, cutoff, zero = lax.optimization_barrier((to_chip, to_core, cutoff, jnp.int32(0)))
     pairs = [(i, i + 1 if i % 2 else i - 1) for i in range(1, bands - 1)]
     chip = lax.ppermute(to_chip, "band", pairs)
     core = lax.ppermute(to_core, "band", [(i, i ^ 1) for i in range(bands)])
     (own,) = tile_sums(got, (1,))
+    tables = zonal_tables(cutoff, zero)
+    own, *tables = lax.optimization_barrier((own, *tables))
     rows = by_row(own, core, chip)
     remapped = by_latitude(rows)
     rows, remapped = lax.optimization_barrier((exchange(rows), remapped))
-    rows = zonal_filter(rows, zonal_tables(cutoff, zero))
+    rows = zonal_filter(rows, tables)
     filtered = by_latitude(exchange(rows))
     return (remapped, filtered)
 

time: 116 us -> 116 us (level)
  waiting for transfers between devices: 17.1 us -> 19.6 us
    ppermute x1, waiting for transfers between devices: 3.41 us -> 5.77 us  [local(): chip = lax.ppermute(to_chip, 'band', pairs)]
    concatenate x2 -> x0, local copies, waits for them, and re-layouts: 1.27 us -> none  [the longest x1 1.18 us: zonal_tables(): g = jnp.concatenate([three(gt.T, 0)] * 3, axis=1)]
  transfers between devices with their start and end apart: 3 -> 3, of which waited for: 2 -> 2; matrix products, arithmetic and copies ran while one was open for 3% -> 1% of each run, Pallas kernels for 2% -> 2%
where the time goes in v1:
time: 116 us; the launch traced here: 115 us
  blocking collectives  75.5 us (65%)
  waiting for transfers between devices  19.6 us (17%)
  Pallas kernels  10.9 us (9%)
  starting transfers between devices  7.2 us (6%)
    all_to_all x2, blocking collectives, exchange(): return lax.all_to_all(array, 'col', 0, 0, tiled=True)  75.5 us
    all_to_all x1, waiting for transfers between devices, exchange(): return lax.all_to_all(array, 'col', 0, 0, tiled=True)  13.9 us
    ppermute x1, waiting for transfers between devices, local(): chip = lax.ppermute(to_chip, 'band', pairs)  5.77 us
    pallas_call x1, Pallas kernels, place(): pl.pallas_call(place_kernel, out_shape=pltpu.VMEM((COLS, ROWS, BLK), jnp....  4.98 us
    all_to_all x1, starting transfers between devices, exchange(): return lax.all_to_all(array, 'col', 0, 0, tiled=True)  4.73 us
    pallas_call x2, Pallas kernels, by_latitude(): pl.pallas_call(lay_kernel, out_shape=jax.ShapeDtypeStruct((LEV, LATB, LON...  2.7 us
    ppermute x1, starting transfers between devices, local(): chip = lax.ppermute(to_chip, 'band', pairs)  2.45 us
  transfers between devices with their start and end apart: 3, of which 2 were waited for; matrix products, arithmetic and copies ran while one was open for 1% of the time, Pallas kernels for 2%

profile of v1, /device:TPU:8, one launch (start us, length us, event | category | flops | bytes accessed | tf_op | source)
XLA Modules:
  0.0 115.5 jit_solution(6782982789636414489)
XLA Ops:
  0.6 5.0 %place.1 = f32[32,112,128]{2,1,0:T(8,128)S(1)} custom-call(s32[256]{0:T(256)} %sb_hbm.1, s32[256]{0:T(256)} %bitcast.17, s32[256]{0:T(256)} %tile_hbm.1, bf16[6,16384]{1,0:T(8,128)(2,1)} %src_hbm.1, bf16[256,128,128]{2,1,0:T(8,128)(2,1)} %w_hbm.1), custom_call_target="tpu_custom_call" | custom-call | flops 100000000 | bytes 10000000 | tf_op jit(solution)/shard_map/place/pallas_call | solution.py:94
  5.6 56.9 %all_to_all.15 = f32[32,112,128]{2,1,0:T(8,128)S(1)} all-to-all(f32[32,112,128]{2,1,0:T(8,128)S(1)} %place.1), channel_id=1, replica_groups=mesh['band'=8,'col'=32] {'col'}, dimensions={0} | all-to-all | bytes 3670016 | tf_op jit(solution)/shard_map/all_to_all | solution.py:267
  62.5 0.0 copy-start
  62.5 0.4 shard_map.78
  62.9 0.1 fusion.22
  63.0 0.1 reduce-precision_convert_fusion.2
  63.1 0.2 fusion.6
  63.3 0.2 sine_select_fusion
  63.5 0.1 mul.58
  63.6 0.1 iota.62
  63.7 0.0 copy-done
  63.7 0.1 le.13
  63.8 0.1 le.14
  63.9 0.0 collective-permute-start
  63.9 2.4 %collective-permute-start.1 = (f32[720,128]{1,0:T(8,128)S(1)}, f32[720,128]{1,0:T(8,128)S(1)}, u32[]{:S(2)}, u32[]{:S(2)}) collective-permute-start(f32[720,128]{1,0:T(8,128)S(1)} %get-tuple-element.24), channel_id=1, source_target_pairs={{32,64},{64,32},{96,128},{128,96},{160,192},{192,160},{33,65},{65,... | collective-permute-start | bytes 1105928 | tf_op jit(solution)/shard_map/ppermute | solution.py:277
  66.4 0.2 multiply_select_fusion.gain_ref
  66.5 0.1 pad_maximum_fusion.3.ft_ref
  66.6 0.3 shard_map.77.own_ref
  67.0 0.0 collective-permute-done.core_ref
  67.0 5.8 %collective-permute-done.1.chip_ref = f32[720,128]{1,0:T(8,128)S(1)} collective-permute-done((f32[720,128]{1,0:T(8,128)S(1)}, f32[720,128]{1,0:T(8,128)S(1)}, u32[]{:S(2)}, u32[]{:S(2)}) %collective-permute-start.1) | collective-permute-done | bytes 368672 | tf_op jit(solution)/shard_map/ppermute | solution.py:277
  72.7 1.1 by_row.1
  73.8 4.7 %all-to-all-start.1 = ((f32[32,24,128]{2,1,0:T(8,128)}), f32[32,24,128]{2,1,0:T(8,128)S(1)}, u32[]{:S(2)}, u32[]{:S(2)}) async-start(f32[32,24,128]{2,1,0:T(8,128)} %by_row.1), calls=%async_computation.1 | async-start | bytes 786432 | tf_op jit(solution)/shard_map/all_to_all | solution.py:267
  78.6 0.1 copy.10.f_ref
  78.7 0.2 copy.11.g_ref
  78.9 1.8 %lay.2 = f32[6,64,225]{2,1,0:T(8,128)} custom-call(f32[768,128]{1,0:T(8,128)} %bitcast.4.rows_ref), custom_call_target="tpu_custom_call" | custom-call | flops 1000000 | bytes 800000 | tf_op jit(solution)/shard_map/lay/pallas_call | solution.py:255
  80.8 13.9 %all-to-all-done.1 = f32[32,24,128]{2,1,0:T(8,128)S(1)} async-done(((f32[32,24,128]{2,1,0:T(8,128)}), f32[32,24,128]{2,1,0:T(8,128)S(1)}, u32[]{:S(2)}, u32[]{:S(2)}) %all-to-all-start.1) | async-done | bytes 393248 | tf_op jit(solution)/shard_map/all_to_all | solution.py:267
  94.6 1.4 %zonal.1 = f32[768,128]{1,0:T(8,128)S(1)} custom-call(f32[768,128]{1,0:T(8,128)S(1)} %bitcast.15, bf16[64,96]{1,0:T(8,128)(2,1)S(1)} %copy.10.f_ref, bf16[32,192]{1,0:T(8,128)(2,1)S(1)} %pad_maximum_fusion.3.ft_ref, bf16[1536,96]{1,0:T(8,128)(2,1)S(1)} %copy.11.g_ref, bf16[96,512]{1,0:T(8,128)(2,1)S(1)} %pad_maximum_fusion.gt_ref, ...), custom_call_target="tpu_custom_call" | custom-call | flops 300000000 | bytes 1000000 | tf_op jit(solution)/shard_map/zonal/pallas_call | solution.py:203
  96.0 18.6 %all_to_all.16 = f32[32,24,128]{2,1,0:T(8,128)S(1)} all-to-all(f32[32,24,128]{2,1,0:T(8,128)S(1)} %bitcast.16), channel_id=1, replica_groups=mesh['band'=8,'col'=32] {'col'}, dimensions={0} | all-to-all | bytes 786432 | tf_op jit(solution)/shard_map/all_to_all | solution.py:267
  114.6 0.8 lay.3
  (12 shorter events, 0.1 us)
Async XLA Ops:
  62.5 1.2 %copy-start = (s32[2]{0:T(128)S(1)}, s32[2]{0:T(128)}, u32[]{:S(2)}) copy-start(s32[2]{0:T(128)} %param.11) | copy-start | bytes 28
  63.9 3.1 %collective-permute-start = (f32[720,128]{1,0:T(8,128)S(1)}, f32[720,128]{1,0:T(8,128)S(1)}, u32[]{:S(2)}, u32[]{:S(2)}) collective-permute-start(f32[720,128]{1,0:T(8,128)S(1)} %get-tuple-element.23), channel_id=1, source_target_pairs={{0,32},{32,0},{64,96},{96,64},{128,160},{160,128},{192,224},{224,1... | collective-permute-start | bytes 1105928 | tf_op jit(solution)/shard_map/ppermute | solution.py:278
  63.9 8.8 %collective-permute-start.1 = (f32[720,128]{1,0:T(8,128)S(1)}, f32[720,128]{1,0:T(8,128)S(1)}, u32[]{:S(2)}, u32[]{:S(2)}) collective-permute-start(f32[720,128]{1,0:T(8,128)S(1)} %get-tuple-element.24), channel_id=1, source_target_pairs={{32,64},{64,32},{96,128},{128,96},{160,192},{192,160},{33,65},{65,... | collective-permute-start | bytes 1105928 | tf_op jit(solution)/shard_map/ppermute | solution.py:277
  73.8 20.8 %all-to-all-start.1 = ((f32[32,24,128]{2,1,0:T(8,128)}), f32[32,24,128]{2,1,0:T(8,128)S(1)}, u32[]{:S(2)}, u32[]{:S(2)}) async-start(f32[32,24,128]{2,1,0:T(8,128)} %by_row.1), calls=%async_computation.1 | async-start | bytes 786432 | tf_op jit(solution)/shard_map/all_to_all | solution.py:267

commit v2 on v1

--- a/solution.py
+++ b/solution.py
@@ -21,6 +21,7 @@
 WINDOW = 8
 TILES = 120
 P2_ROWS = 24
+PART = 8
 CHUNK = 128
 CHUNKS = 2
 AXES = True
@@ -144,7 +145,11 @@
     )(got)
 
 
-def by_row_kernel(own_ref, core_ref, chip_ref, out_ref, sums):
+def by_row_kernel(own_ref, core_ref, chip_ref, out_hbm, sums, out_ref, sem):
+    def part_copy(i):
+        part = pl.ds(i * PART, PART)
+        return pltpu.make_async_copy(out_ref.at[part], out_hbm.at[part], sem.at[i])
+
     sums[...] = own_ref[...] + core_ref[...] + chip_ref[...]
     lane = lax.broadcasted_iota(jnp.int32, (LEV, BLK), 1)
     for lat in range(LATB):
@@ -156,13 +161,22 @@
                 value = jnp.where(lane < BLK - shift, pltpu.roll(value, BLK - shift, 1), pltpu.roll(later, BLK - shift, 1))
             at = (lat % 2) * 2 * LEV + half * LEV
             out_ref[lat // 2, at : at + LEV, :] = value
+        if (lat + 1) % (2 * PART) == 0:
+            part_copy(lat // (2 * PART)).start()
+    for i in range(COLS // PART):
+        part_copy(i).wait()
 
 
 def by_row(own, core, chip, interpret=False):
     return pl.pallas_call(
         by_row_kernel,
         out_shape=jax.ShapeDtypeStruct((COLS, P2_ROWS, BLK), jnp.float32),
-        scratch_shapes=[pltpu.VMEM((LEV * TILES, BLK), jnp.float32)],
+        out_specs=pl.BlockSpec(memory_space=pltpu.HBM),
+        scratch_shapes=[
+            pltpu.VMEM((LEV * TILES, BLK), jnp.float32),
+            pltpu.VMEM((COLS, P2_ROWS, BLK), jnp.float32),
+            pltpu.SemaphoreType.DMA((COLS // PART,)),
+        ],
         compiler_params=pltpu.CompilerParams(vmem_limit_bytes=12 << 20),
         cost_estimate=pl.CostEstimate(flops=1_000_000, bytes_accessed=1_500_000, transcendentals=0),
         interpret=interpret,
@@ -240,22 +254,27 @@
     return three(f, 1), three(f.T, 1), g, three(gt, 0), tc, ts, gain
 
 
-def lay_kernel(rows_ref, out_ref, low, high):
-    for h, half in enumerate((low, high)):
-        for p in range(2):
-            for l in range(LEV):
+def lay_kernel(rows_ref, out_hbm, low, high, out_ref, sem):
+    copies = [pltpu.make_async_copy(out_ref.at[l], out_hbm.at[l], sem.at[l]) for l in range(LEV)]
+    for l in range(LEV):
+        for h, half in enumerate((low, high)):
+            for p in range(2):
                 part = rows_ref[pl.ds(p * 2 * LEV + h * LEV + l, COLS, stride=P2_ROWS), :]
                 half[pl.ds(l * LATB + p, COLS, stride=2), :] = part
-    for l in range(LEV):
         out_ref[l, :, :BLK] = low[l * LATB : l * LATB + LATB, :]
         out_ref[l, :, BLK:] = high[l * LATB : l * LATB + LATB, : LON - BLK]
+        copies[l].start()
+    for copy in copies:
+        copy.wait()
 
 
 def by_latitude(rows, interpret=False):
     return pl.pallas_call(
         lay_kernel,
         out_shape=jax.ShapeDtypeStruct((LEV, LATB, LON), jnp.float32),
-        scratch_shapes=[pltpu.VMEM((LEV * LATB, BLK), jnp.float32)] * 2,
+        out_specs=pl.BlockSpec(memory_space=pltpu.HBM),
+        scratch_shapes=[pltpu.VMEM((LEV * LATB, BLK), jnp.float32)] * 2
+        + [pltpu.VMEM((LEV, LATB, LON), jnp.float32), pltpu.SemaphoreType.DMA((LEV,))],
         cost_estimate=pl.CostEstimate(flops=1_000_000, bytes_accessed=800_000, transcendentals=0),
         compiler_params=pltpu.CompilerParams(vmem_limit_bytes=8 << 20),
         interpret=interpret,

time: 116 us -> 116 us (level)
  no operation moved by 1% of the time
where the time goes in v2:
time: 116 us; the launch traced here: 115 us
  blocking collectives  75.5 us (65%)
  waiting for transfers between devices  19.7 us (17%)
  Pallas kernels  10.7 us (9%)
  starting transfers between devices  7.22 us (6%)
    all_to_all x2, blocking collectives, exchange(): return lax.all_to_all(array, 'col', 0, 0, tiled=True)  75.5 us
    all_to_all x1, waiting for transfers between devices, exchange(): return lax.all_to_all(array, 'col', 0, 0, tiled=True)  13.9 us
    ppermute x1, waiting for transfers between devices, local(): chip = lax.ppermute(to_chip, 'band', pairs)  5.77 us
    pallas_call x1, Pallas kernels, place(): pl.pallas_call(place_kernel, out_shape=pltpu.VMEM((COLS, ROWS, BLK), jnp....  4.98 us
    all_to_all x1, starting transfers between devices, exchange(): return lax.all_to_all(array, 'col', 0, 0, tiled=True)  4.74 us
    pallas_call x2, Pallas kernels, by_latitude(): pl.pallas_call(lay_kernel, out_shape=jax.ShapeDtypeStruct((LEV, LATB, LON...  2.62 us
    ppermute x1, starting transfers between devices, local(): chip = lax.ppermute(to_chip, 'band', pairs)  2.45 us
  transfers between devices with their start and end apart: 3, of which 2 were waited for; matrix products, arithmetic and copies ran while one was open for 1% of the time, Pallas kernels for 2%

profile of v2, /device:TPU:8, one launch (start us, length us, event | category | flops | bytes accessed | tf_op | source)
XLA Modules:
  0.0 115.4 jit_solution(11340492302637923809)
XLA Ops:
  0.6 5.0 %place.1 = f32[32,112,128]{2,1,0:T(8,128)S(1)} custom-call(s32[256]{0:T(256)} %sb_hbm.1, s32[256]{0:T(256)} %bitcast.17, s32[256]{0:T(256)} %tile_hbm.1, bf16[6,16384]{1,0:T(8,128)(2,1)} %src_hbm.1, bf16[256,128,128]{2,1,0:T(8,128)(2,1)} %w_hbm.1), custom_call_target="tpu_custom_call" | custom-call | flops 100000000 | bytes 10000000 | tf_op jit(solution)/shard_map/place/pallas_call | solution.py:95
  5.6 56.9 %all_to_all.15 = f32[32,112,128]{2,1,0:T(8,128)S(1)} all-to-all(f32[32,112,128]{2,1,0:T(8,128)S(1)} %place.1), channel_id=1, replica_groups=mesh['band'=8,'col'=32] {'col'}, dimensions={0} | all-to-all | bytes 3670016 | tf_op jit(solution)/shard_map/all_to_all | solution.py:286
  62.5 0.0 copy-start
  62.5 0.4 shard_map.78
  62.9 0.1 fusion.22
  63.0 0.1 reduce-precision_convert_fusion.2
  63.1 0.2 fusion.6
  63.3 0.2 sine_select_fusion
  63.5 0.1 mul.58
  63.6 0.1 iota.62
  63.7 0.0 copy-done
  63.7 0.1 le.13
  63.8 0.1 le.14
  63.9 0.0 collective-permute-start
  63.9 2.4 %collective-permute-start.1 = (f32[720,128]{1,0:T(8,128)S(1)}, f32[720,128]{1,0:T(8,128)S(1)}, u32[]{:S(2)}, u32[]{:S(2)}) collective-permute-start(f32[720,128]{1,0:T(8,128)S(1)} %get-tuple-element.24), channel_id=1, source_target_pairs={{32,64},{64,32},{96,128},{128,96},{160,192},{192,160},{33,65},{65,... | collective-permute-start | bytes 1105928 | tf_op jit(solution)/shard_map/ppermute | solution.py:296
  66.4 0.2 multiply_select_fusion.gain_ref
  66.5 0.1 pad_maximum_fusion.3.ft_ref
  66.6 0.3 shard_map.77.own_ref
  67.0 0.0 collective-permute-done.core_ref
  67.0 5.8 %collective-permute-done.1.chip_ref = f32[720,128]{1,0:T(8,128)S(1)} collective-permute-done((f32[720,128]{1,0:T(8,128)S(1)}, f32[720,128]{1,0:T(8,128)S(1)}, u32[]{:S(2)}, u32[]{:S(2)}) %collective-permute-start.1) | collective-permute-done | bytes 368672 | tf_op jit(solution)/shard_map/ppermute | solution.py:296
  72.7 1.0 by_row.1
  73.8 4.7 %all-to-all-start.1 = ((f32[32,24,128]{2,1,0:T(8,128)}), f32[32,24,128]{2,1,0:T(8,128)S(1)}, u32[]{:S(2)}, u32[]{:S(2)}) async-start(f32[32,24,128]{2,1,0:T(8,128)} %by_row.1), calls=%async_computation.1 | async-start | bytes 786432 | tf_op jit(solution)/shard_map/all_to_all | solution.py:286
  78.5 0.1 copy.10.f_ref
  78.6 0.2 copy.11.g_ref
  78.9 1.8 %lay.2 = f32[6,64,225]{2,1,0:T(8,128)} custom-call(f32[768,128]{1,0:T(8,128)} %bitcast.4.rows_ref), custom_call_target="tpu_custom_call" | custom-call | flops 1000000 | bytes 800000 | tf_op jit(solution)/shard_map/lay/pallas_call | solution.py:272
  80.7 13.9 %all-to-all-done.1 = f32[32,24,128]{2,1,0:T(8,128)S(1)} async-done(((f32[32,24,128]{2,1,0:T(8,128)}), f32[32,24,128]{2,1,0:T(8,128)S(1)}, u32[]{:S(2)}, u32[]{:S(2)}) %all-to-all-start.1) | async-done | bytes 393248 | tf_op jit(solution)/shard_map/all_to_all | solution.py:286
  94.6 1.4 %zonal.1 = f32[768,128]{1,0:T(8,128)S(1)} custom-call(f32[768,128]{1,0:T(8,128)S(1)} %bitcast.15, bf16[64,96]{1,0:T(8,128)(2,1)S(1)} %copy.10.f_ref, bf16[32,192]{1,0:T(8,128)(2,1)S(1)} %pad_maximum_fusion.3.ft_ref, bf16[1536,96]{1,0:T(8,128)(2,1)S(1)} %copy.11.g_ref, bf16[96,512]{1,0:T(8,128)(2,1)S(1)} %pad_maximum_fusion.gt_ref, ...), custom_call_target="tpu_custom_call" | custom-call | flops 300000000 | bytes 1000000 | tf_op jit(solution)/shard_map/zonal/pallas_call | solution.py:217
  96.0 18.6 %all_to_all.16 = f32[32,24,128]{2,1,0:T(8,128)S(1)} all-to-all(f32[32,24,128]{2,1,0:T(8,128)S(1)} %bitcast.16), channel_id=1, replica_groups=mesh['band'=8,'col'=32] {'col'}, dimensions={0} | all-to-all | bytes 786432 | tf_op jit(solution)/shard_map/all_to_all | solution.py:286
  114.6 0.8 lay.3
  (12 shorter events, 0.1 us)
Async XLA Ops:
  62.5 1.2 %copy-start = (s32[2]{0:T(128)S(1)}, s32[2]{0:T(128)}, u32[]{:S(2)}) copy-start(s32[2]{0:T(128)} %param.11) | copy-start | bytes 28
  63.9 3.1 %collective-permute-start = (f32[720,128]{1,0:T(8,128)S(1)}, f32[720,128]{1,0:T(8,128)S(1)}, u32[]{:S(2)}, u32[]{:S(2)}) collective-permute-start(f32[720,128]{1,0:T(8,128)S(1)} %get-tuple-element.23), channel_id=1, source_target_pairs={{0,32},{32,0},{64,96},{96,64},{128,160},{160,128},{192,224},{224,1... | collective-permute-start | bytes 1105928 | tf_op jit(solution)/shard_map/ppermute | solution.py:297
  63.9 8.8 %collective-permute-start.1 = (f32[720,128]{1,0:T(8,128)S(1)}, f32[720,128]{1,0:T(8,128)S(1)}, u32[]{:S(2)}, u32[]{:S(2)}) collective-permute-start(f32[720,128]{1,0:T(8,128)S(1)} %get-tuple-element.24), channel_id=1, source_target_pairs={{32,64},{64,32},{96,128},{128,96},{160,192},{192,160},{33,65},{65,... | collective-permute-start | bytes 1105928 | tf_op jit(solution)/shard_map/ppermute | solution.py:296
  73.8 20.8 %all-to-all-start.1 = ((f32[32,24,128]{2,1,0:T(8,128)}), f32[32,24,128]{2,1,0:T(8,128)S(1)}, u32[]{:S(2)}, u32[]{:S(2)}) async-start(f32[32,24,128]{2,1,0:T(8,128)} %by_row.1), calls=%async_computation.1 | async-start | bytes 786432 | tf_op jit(solution)/shard_map/all_to_all | solution.py:286
